TPU v7x, 512 devices: a whole 4x4x16 slice. The times are simulated.
512 devices in a mesh: fsdp: 16 (over x, z_hi), tensor: 8 (over z_lo, core), pool: 4 (over y).
Axes of the slice: x: 4, y: 4, z: 16 (z_hi: 4, z_lo: 4; z = z_hi * 4 + z_lo), core: 2. Of those that a mesh axis runs over, the one named last changes fastest.
Arguments:
- hidden: bfloat16 [32768, 5120], P(('fsdp', 'pool'), 'tensor'), may hold values from -6 to 6
- queries: bfloat16 [32768, 5120], P(('fsdp', 'pool'), 'tensor'), may hold values from -200 to 200
- cotangent: bfloat16 [32768, 5120], P(('fsdp', 'pool'), 'tensor'), may hold values from -6 to 6
- segment: int32 [64, 512], P(('fsdp', 'pool')), may hold values from 0 to 15, never falling along the last dimension, each value on 1 to 384 neighbouring positions
- clip_mask: int32 [32768], P(('fsdp', 'pool')), may hold values 0 or 1
- rewards: float32 [1024], P(('fsdp', 'pool')), may hold values from 0 to 1
- seq_order: int32 [1024], P(('fsdp', 'pool')), may hold values from 0 to 1023, each once
- kv_weight: float32 [5120, 2, 1024], P('fsdp', None, 'tensor'), may hold values from -0.078125 to 0.078125
- moment_one: float32 [5120, 2, 1024], P('fsdp', None, 'tensor'), may hold values from -60 to 60
- moment_two: float32 [5120, 2, 1024], P('fsdp', None, 'tensor'), may hold values from 1 to 10000
- dec_hidden: bfloat16 [512, 4, 5120], P(('fsdp', 'pool')), may hold values from -6 to 6
- dec_queries: bfloat16 [512, 4, 5120], P(('fsdp', 'pool'), None, 'tensor'), may hold values from -200 to 200
- kv_cache: bfloat16 [512, 256, 2, 1024], P(('fsdp', 'pool'), None, None, 'tensor'), may hold values from -6 to 6
- cache_len: int32 [512], P(('fsdp', 'pool')), may hold values from 1 to 256
Outputs:
- new_weight: float32 [5120, 2, 1024], P('fsdp', None, 'tensor')
- new_moment_one: float32 [5120, 2, 1024], P('fsdp', None, 'tensor')
- new_moment_two: float32 [5120, 2, 1024], P('fsdp', None, 'tensor')
- dec_out: bfloat16 [512, 4, 5120], P(('fsdp', 'pool'), None, 'tensor')
Inputs may be any that keep to these rules, and one draw needn't show every extreme that they name: `segment`: each row never falls; every sequence number of a row has 1 to 384 tokens. `seq_order`: each place once.
All inputs are finite; a program needn't handle non-finite values. No bound on the sum of `clip_mask` on one device may be relied on, other than what follows from the above.
Results may differ from a plain program's by a relative error of at most 0.014.
The roundings to bfloat16 on the way count: a program that leaves them out, or rounds other values in their place, can miss the bound.
Values may be sent and summed in bfloat16 or wider, within the bound.
A program may use at most 64 MiB of HBM per device.

v0:
```python
import math
import jax
import jax.numpy as jnp
from jax import lax
from jax.sharding import Mesh
from jax.sharding import PartitionSpec as P

D = 5120
QH = 40
KVH = 8
HD = 128
GROUP = 16
FSDP = ("fsdp_0", "fsdp_1")
FSDP_POOL = ("fsdp_0", "fsdp_1", "pool")
beta_one = 0.9
beta_two = 0.999
learn_rate = 0.001
weight_decay = 0.1
adam_epsilon = 1e-08
adam_step = 10.0
variance_floor = 0.04
masked_score = -1e30


def from_everyone(shard, axis):
    count = lax.axis_size(axis)
    return lax.all_to_all(
        jnp.broadcast_to(shard[None], (count, *shard.shape)), axis, 0, 0, tiled=True
    )


def of_everyone(shard, axis):
    everything = from_everyone(shard, axis)
    return jnp.sum(everything, axis=0)


def sum_by_axis(terms, axes):
    so_far = terms.astype(jnp.bfloat16)
    for axis in axes:
        so_far = lax.psum_scatter(so_far, axis, scatter_dimension=0, tiled=True)
    return so_far.astype(jnp.float32)


def cut_along(shard, dim, count):
    before, after = (shard.shape[:dim], shard.shape[dim + 1 :])
    return jnp.moveaxis(shard.reshape(*before, count, -1, *after), dim, 0)


def summed_on_arrival(shard, axis, dim):
    pieces = cut_along(shard, dim, lax.axis_size(axis))
    arrived = lax.all_to_all(pieces, axis, split_axis=0, concat_axis=0, tiled=True)
    return arrived.sum(axis=0)


def learner_grads(keys_values, queries, cotangent, segment, coefficient):
    block_rows = queries.shape[0]
    head_size = queries.shape[3]
    score_scale = 1.0 / math.sqrt(head_size)
    key_rows = keys_values[:, 0]
    value_rows = keys_values[:, 1]
    scores = (
        jnp.einsum("thrd,uhd->hrtu", queries, key_rows, preferred_element_type=jnp.float32)
        * score_scale
    )
    places = jnp.arange(block_rows)
    allowed = (segment[:, None] == segment[None, :]) & (places[None, :] <= places[:, None])
    scores = jnp.where(allowed, scores, masked_score)
    row_max = jnp.max(scores, axis=-1, keepdims=True)
    weights = jnp.exp(scores - row_max)
    attention = weights / jnp.sum(weights, axis=-1, keepdims=True)
    attention_low = attention.astype(jnp.bfloat16)
    upstream = (coefficient[:, None, None, None] * cotangent.astype(jnp.float32)).astype(
        jnp.bfloat16
    )
    grad_prob = jnp.einsum(
        "thrd,uhd->hrtu", upstream, value_rows, preferred_element_type=jnp.float32
    )
    row_inner = jnp.sum(attention * grad_prob, axis=-1, keepdims=True)
    grad_score = (attention * (grad_prob - row_inner) * score_scale).astype(jnp.bfloat16)
    grad_values = jnp.einsum(
        "hrtu,thrd->uhd", attention_low, upstream, preferred_element_type=jnp.float32
    )
    grad_keys = jnp.einsum(
        "hrtu,thrd->uhd", grad_score, queries, preferred_element_type=jnp.float32
    )
    return jnp.stack([grad_keys, grad_values], axis=1).astype(jnp.bfloat16)


def decode_attend(queries, cache, fresh, lengths):
    head_size = queries.shape[4]
    steps_here = queries.shape[1]
    capacity = cache.shape[1]
    score_scale = 1.0 / math.sqrt(head_size)
    cached = (
        jnp.einsum("bshqd,blhd->bshql", queries, cache[:, :, 0], preferred_element_type=jnp.float32)
        * score_scale
    )
    recent = (
        jnp.einsum("bshqd,bjhd->bshqj", queries, fresh[:, :, 0], preferred_element_type=jnp.float32)
        * score_scale
    )
    live = jnp.arange(capacity)[None, :] < lengths[:, None]
    cached = jnp.where(live[:, None, None, None, :], cached, masked_score)
    before = jnp.arange(steps_here)[None, :] <= jnp.arange(steps_here)[:, None]
    recent = jnp.where(before[None, :, None, None, :], recent, masked_score)
    row_max = jnp.maximum(
        jnp.max(cached, axis=-1, keepdims=True), jnp.max(recent, axis=-1, keepdims=True)
    )
    cached_exp = jnp.exp(cached - row_max)
    recent_exp = jnp.exp(recent - row_max)
    total = jnp.sum(cached_exp, axis=-1, keepdims=True) + jnp.sum(
        recent_exp, axis=-1, keepdims=True
    )
    cached_low = (cached_exp / total).astype(jnp.bfloat16)
    recent_low = (recent_exp / total).astype(jnp.bfloat16)
    output = jnp.einsum(
        "bshql,blhd->bshqd", cached_low, cache[:, :, 1], preferred_element_type=jnp.float32
    )
    output = output + jnp.einsum(
        "bshqj,bjhd->bshqd", recent_low, fresh[:, :, 1], preferred_element_type=jnp.float32
    )
    return output.astype(jnp.bfloat16).reshape(queries.shape[0], steps_here, -1)


def body(
    hidden,
    queries,
    cotangent,
    segment,
    clip_mask,
    rewards,
    seq_order,
    kv_weight,
    moment_one,
    moment_two,
    dec_hidden,
    dec_queries,
    kv_cache,
    cache_len,
):
    block_rows = hidden.shape[0]
    kv_width = kv_weight.shape[2]
    heads_here = kv_width // HD
    head_ratio = QH // KVH
    weight_low = kv_weight.astype(jnp.bfloat16)
    weight_full = lax.all_gather(weight_low, FSDP, axis=0, tiled=True)
    tokens_full = lax.all_gather(hidden, "tensor", axis=1, tiled=True)
    projected = jnp.dot(
        tokens_full, weight_full.reshape(D, 2 * kv_width), preferred_element_type=jnp.float32
    )
    keys_values = projected.astype(jnp.bfloat16).reshape(block_rows, 2, heads_here, HD)
    shards = lax.axis_size(FSDP) * lax.axis_size("pool")
    groups_total = rewards.shape[0] * shards // GROUP
    group_of = seq_order // GROUP
    onehot = (group_of[:, None] == jnp.arange(groups_total, dtype=jnp.int32)[None, :]).astype(
        jnp.float32
    )
    stats = jnp.stack([rewards, rewards * rewards], axis=1)
    partial_sums = jnp.sum(onehot[:, :, None] * stats[:, None, :], axis=0)
    sums = of_everyone(partial_sums, FSDP_POOL)
    mean = sums[:, 0] / GROUP
    spread = sums[:, 1] / GROUP - mean * mean
    denom = jnp.sqrt(jnp.maximum(spread, variance_floor))
    advantage = (rewards - jnp.sum(onehot * mean[None, :], axis=1)) / jnp.sum(
        onehot * denom[None, :], axis=1
    )
    local_seg = segment[0]
    member = (local_seg[:, None] == jnp.arange(rewards.shape[0], dtype=jnp.int32)[None, :]).astype(
        jnp.float32
    )
    coefficient = jnp.sum(member * advantage[None, :], axis=1) * clip_mask.astype(jnp.float32)
    query_rows = queries.reshape(block_rows, heads_here, head_ratio, HD)
    cot_rows = cotangent.reshape(block_rows, heads_here, head_ratio, HD)
    grad_kv = learner_grads(keys_values, query_rows, cot_rows, local_seg, coefficient).reshape(
        block_rows, 2 * kv_width
    )
    partial_value = jnp.einsum(
        "tc,tk->ck", tokens_full, grad_kv, preferred_element_type=jnp.float32
    )
    shard_grad = sum_by_axis(
        partial_value.reshape(kv_weight.shape[0] * lax.axis_size(FSDP), 2, kv_width), FSDP
    )
    grad = of_everyone(shard_grad, "pool")
    new_moment_one = beta_one * moment_one + (1.0 - beta_one) * grad
    new_moment_two = beta_two * moment_two + (1.0 - beta_two) * grad * grad
    first_hat = new_moment_one / (1.0 - beta_one**adam_step)
    second_hat = new_moment_two / (1.0 - beta_two**adam_step)
    new_weight = kv_weight - learn_rate * (
        first_hat / (jnp.sqrt(second_hat) + adam_epsilon) + weight_decay * kv_weight
    )
    dec_rows = dec_hidden.shape[0]
    steps_here = dec_hidden.shape[1]
    capacity = kv_cache.shape[1]
    rollout_low = new_weight.astype(jnp.bfloat16)
    columns = lax.all_to_all(dec_hidden, FSDP, split_axis=2, concat_axis=0, tiled=True)
    piece_width = columns.shape[2]
    rollout_flat = rollout_low.reshape(piece_width, 2 * kv_width)
    product = jnp.dot(
        columns.reshape(dec_rows * lax.axis_size(FSDP) * steps_here, piece_width),
        rollout_flat,
        preferred_element_type=jnp.float32,
    )
    fresh = summed_on_arrival(
        product.reshape(dec_rows * lax.axis_size(FSDP), steps_here, 2 * kv_width), FSDP, 0
    )
    fresh_low = fresh.astype(jnp.bfloat16).reshape(dec_rows, steps_here, 2, heads_here, HD)
    cache = kv_cache.reshape(dec_rows, capacity, 2, heads_here, HD)
    query_dec = dec_queries.reshape(dec_rows, steps_here, heads_here, head_ratio, HD)
    dec_out = decode_attend(query_dec, cache, fresh_low, cache_len)
    return (new_weight, new_moment_one, new_moment_two, dec_out)


def solution(mesh):
    finer = Mesh(
        mesh.devices.reshape(4, 4, mesh.shape["tensor"], mesh.shape["pool"]),
        ("fsdp_0", "fsdp_1", "tensor", "pool"),
    )
    in_specs = (
        P(FSDP_POOL, "tensor"),
        P(FSDP_POOL, "tensor"),
        P(FSDP_POOL, "tensor"),
        P(FSDP_POOL, None),
        P(FSDP_POOL),
        P(FSDP_POOL),
        P(FSDP_POOL),
        P(FSDP, None, "tensor"),
        P(FSDP, None, "tensor"),
        P(FSDP, None, "tensor"),
        P(FSDP_POOL, None, None),
        P(FSDP_POOL, None, "tensor"),
        P(FSDP_POOL, None, None, "tensor"),
        P(FSDP_POOL),
    )
    out_specs = (
        P(FSDP, None, "tensor"),
        P(FSDP, None, "tensor"),
        P(FSDP, None, "tensor"),
        P(FSDP_POOL, None, "tensor"),
    )
    return jax.shard_map(body, mesh=finer, in_specs=in_specs, out_specs=out_specs, check_vma=False)
```

profile of v0, /device:TPU:1, one launch (start us, length us, event | category | flops | bytes accessed | tf_op | source)
XLA Modules:
  0.0 462.3 jit_solution(10101156402707544405)
XLA Ops:
  7.2 1.8 convert_element_type.98
  12.6 21.7 %all-to-all-start = ((f32[64,1,128]{2,1,0:T(1,128)}), f32[64,1,128]{2,1,0:T(1,128)S(1)}, u32[]{:S(2)}, u32[]{:S(2)}) async-start(f32[64,1,128]{2,1,0:T(1,128)} %reshape.300), calls=%async_computation | async-start | bytes 65536 | tf_op jit(solution)/shard_map/all_to_all | solution.py:27
  38.1 11.9 %all-to-all-done = f32[64,1,128]{2,1,0:T(1,128)S(1)} async-done(((f32[64,1,128]{2,1,0:T(1,128)}), f32[64,1,128]{2,1,0:T(1,128)S(1)}, u32[]{:S(2)}, u32[]{:S(2)}) %all-to-all-start) | async-done | bytes 32800 | tf_op jit(solution)/shard_map/all_to_all | solution.py:27
  53.8 68.1 %all-gather.5.cloned.1.call-done = bf16[5120,2,128]{2,1,0:T(2,128)(2,1)} async-done(((bf16[320,2,128]{2,1,0:T(2,128)(2,1)}), bf16[5120,2,128]{2,1,0:T(2,128)(2,1)}) %all-gather.5.cloned.1.call-update) | async-done | bytes 2621456 | tf_op jit(solution)/shard_map/all_gather | solution.py:146
  122.0 66.0 %all-gather.3.cloned.1.call-done = bf16[512,5120]{1,0:T(8,128)(2,1)} async-done(((bf16[512,640]{1,0:T(8,128)(2,1)}), bf16[512,5120]{1,0:T(8,128)(2,1)}) %all-gather.3.cloned.1.call-update) | async-done | bytes 5242896 | tf_op jit(solution)/shard_map/all_gather | solution.py:147
  187.9 4.9 %fusion.20 = bf16[512,256]{0,1:T(8,128)(2,1)S(1)} fusion(bf16[512,5120]{1,0:T(8,128)(2,1)} %all-gather.3.cloned.1.call-done, bf16[640,8,2,128]{3,2,1,0:T(2,128)(2,1)} %bitcast.254), kind=kOutput, calls=%fused_computation.25 | convolution fusion | flops 1342308352 | bytes 8126464 | tf_op jit(solution)/shard_map/dot_general | solution.py:148
  195.0 1.7 fusion.39
  196.7 1.9 fusion
  198.6 2.4 fusion.42
  201.2 1.6 convolution_convert_fusion
  202.8 4.7 %copy.161 = bf16[5120,2,128]{2,1,0:T(2,128)(2,1)} copy(bf16[5120,2,128]{0,2,1:T(8,128)(2,1)S(1)} %bitcast.240) | data formatting | bytes 5242880 | tf_op jit(solution)/shard_map/convert_element_type | solution.py:38
  207.5 5.0 %copy.170 = bf16[8,4,5120]{0,1,2:T(4,128)(2,1)} copy(bf16[8,4,5120]{2,1,0:T(4,128)(2,1)S(1)} %copy-done.3) | data formatting | bytes 655360 | tf_op args[10]
  212.5 12.3 %reshape.302 = bf16[16,2,5120]{2,1,0:T(2,128)(2,1)} reshape(bf16[5120,4,8]{2,1,0:T(4,128)(2,1)} %bitcast.237) | data formatting | bytes 655360
  224.8 14.2 %all-to-all-start.2 = ((bf16[16,2,5120]{2,1,0:T(2,128)(2,1)}), bf16[16,2,5120]{2,1,0:T(2,128)(2,1)S(1)}, u32[]{:S(2)}, u32[]{:S(2)}) async-start(bf16[16,2,5120]{2,1,0:T(2,128)(2,1)} %reshape.302), calls=%async_computation.2 | async-start | bytes 655360 | tf_op jit(solution)/shard_map/all_to_all | solution.py:195
  241.0 52.4 %all-reduce.5.cloned.1.call-done = bf16[5120,2,128]{2,1,0:T(2,128)(2,1)} async-done(((bf16[5120,2,128]{2,1,0:T(2,128)(2,1)}), bf16[5120,2,128]{2,1,0:T(2,128)(2,1)}) %all-reduce.5.cloned.1.call-update) | async-done | bytes 2621456
  293.4 2.2 constant_dynamic-slice_fusion.1
  297.5 91.8 %all-reduce.7.cloned.1.call-done = bf16[1280,2,128]{2,1,0:T(2,128)(2,1)} async-done(((bf16[1280,2,128]{2,1,0:T(2,128)(2,1)}), bf16[1280,2,128]{2,1,0:T(2,128)(2,1)}) %all-reduce.7.cloned.1.call-update) | async-done | bytes 655376
  391.6 5.3 %all-to-all-start.1 = ((f32[4,320,2,128]{3,1,2,0:T(8,128)}), f32[4,320,2,128]{3,1,2,0:T(8,128)S(1)}, u32[]{:S(2)}, u32[]{:S(2)}) async-start(f32[4,320,2,128]{3,1,2,0:T(8,128)} %broadcast_in_dim.31), calls=%async_computation.1 | async-start | bytes 2621440 | tf_op jit(solution)/shard_map/all_to_all | solution.py:27
  396.9 7.2 %reshape.303 = bf16[5120,4,8]{2,1,0:T(4,128)(2,1)} reshape(bf16[16,2,5120]{2,1,0:T(2,128)(2,1)S(1)} %all-to-all-done.2) | data formatting | bytes 655360
  404.1 7.0 %copy.171 = bf16[8,4,16,320]{3,1,0,2:T(4,128)(2,1)S(1)} copy(bf16[8,4,16,320]{0,1,3,2:T(4,128)(2,1)} %bitcast.236) | data formatting | bytes 655360 | tf_op jit(solution)/shard_map/all_to_all | solution.py:195
  411.4 2.6 all-to-all-done.1
  415.8 6.7 %all-to-all-start.3 = ((f32[16,8,4,256]{3,2,1,0:T(4,128)}), f32[16,8,4,256]{3,2,1,0:T(4,128)S(1)}, u32[]{:S(2)}, u32[]{:S(2)}) async-start(f32[16,8,4,256]{3,2,1,0:T(4,128)} %reshape_reshape.3), calls=%async_computation.3 | async-start | bytes 1048576 | tf_op jit(solution)/shard_map/all_to_all | solution.py:51
  422.6 1.4 copy.229
  427.4 26.3 %all-to-all-done.3 = f32[16,8,4,256]{3,2,1,0:T(4,128)S(1)} async-done(((f32[16,8,4,256]{3,2,1,0:T(4,128)}), f32[16,8,4,256]{3,2,1,0:T(4,128)S(1)}, u32[]{:S(2)}, u32[]{:S(2)}) %all-to-all-start.3) | async-done | bytes 524320 | tf_op jit(solution)/shard_map/all_to_all | solution.py:51
  (79 shorter events, 25.8 us)
Async XLA Ops:
  7.2 114.8 %all-gather.5.cloned.1.call-start = ((), (), s32[]{:S(2)}) async-start(), calls=%async_computation.5 | async-start | bytes 2785280 | tf_op jit(solution)/shard_map/all_gather | solution.py:146
  9.0 179.0 %all-gather.3.cloned.1.call-start = ((), (), s32[]{:S(2)}) async-start(), calls=%async_computation.4 | async-start | bytes 5898240 | tf_op jit(solution)/shard_map/all_gather | solution.py:147
  12.6 37.3 %all-to-all-start = ((f32[64,1,128]{2,1,0:T(1,128)}), f32[64,1,128]{2,1,0:T(1,128)S(1)}, u32[]{:S(2)}, u32[]{:S(2)}) async-start(f32[64,1,128]{2,1,0:T(1,128)} %reshape.300), calls=%async_computation | async-start | bytes 65536 | tf_op jit(solution)/shard_map/all_to_all | solution.py:27
  34.4 259.0 %all-reduce.5.cloned.1.call-start = ((), (), s32[]{:S(2)}) async-start(), calls=%async_computation.6 | async-start | bytes 5242880
  196.7 4.4 slice-start
  198.6 2.5 slice-start.1
  202.8 4.8 %copy-start.3 = (bf16[8,4,5120]{2,1,0:T(4,128)(2,1)S(1)}, bf16[8,4,5120]{2,1,0:T(4,128)(2,1)}, u32[]{:S(2)}) copy-start(bf16[8,4,5120]{2,1,0:T(4,128)(2,1)} %param.24) | copy-start | bytes 983044
  224.8 165.6 %all-to-all-start.2 = ((bf16[16,2,5120]{2,1,0:T(2,128)(2,1)}), bf16[16,2,5120]{2,1,0:T(2,128)(2,1)S(1)}, u32[]{:S(2)}, u32[]{:S(2)}) async-start(bf16[16,2,5120]{2,1,0:T(2,128)(2,1)} %reshape.302), calls=%async_computation.2 | async-start | bytes 655360 | tf_op jit(solution)/shard_map/all_to_all | solution.py:195
  239.0 150.3 %all-reduce.7.cloned.1.call-start = ((), (), s32[]{:S(2)}) async-start(), calls=%async_computation.7 | async-start | bytes 1310720
  391.6 22.3 %all-to-all-start.1 = ((f32[4,320,2,128]{3,1,2,0:T(8,128)}), f32[4,320,2,128]{3,1,2,0:T(8,128)S(1)}, u32[]{:S(2)}, u32[]{:S(2)}) async-start(f32[4,320,2,128]{3,1,2,0:T(8,128)} %broadcast_in_dim.31), calls=%async_computation.1 | async-start | bytes 2621440 | tf_op jit(solution)/shard_map/all_to_all | solution.py:27
  404.1 9.9 %copy-start = (f32[320,2,128]{2,1,0:T(2,128)S(1)}, f32[320,2,128]{2,1,0:T(2,128)}, u32[]{:S(2)}) copy-start(f32[320,2,128]{2,1,0:T(2,128)} %param.21) | copy-start | bytes 983044
  404.1 9.9 %copy-start.1 = (f32[320,2,128]{2,1,0:T(2,128)S(1)}, f32[320,2,128]{2,1,0:T(2,128)}, u32[]{:S(2)}) copy-start(f32[320,2,128]{2,1,0:T(2,128)} %param.22) | copy-start | bytes 983044
  404.1 9.9 %copy-start.2 = (f32[320,2,128]{2,1,0:T(2,128)S(1)}, f32[320,2,128]{2,1,0:T(2,128)}, u32[]{:S(2)}) copy-start(f32[320,2,128]{2,1,0:T(2,128)} %param.23) | copy-start | bytes 983044
  411.1 11.4 %copy-start.4 = (bf16[8,4,640]{2,1,0:T(4,128)(2,1)S(1)}, bf16[8,4,640]{2,1,0:T(4,128)(2,1)}, u32[]{:S(2)}) copy-start(bf16[8,4,640]{2,1,0:T(4,128)(2,1)} %param.25) | copy-start | bytes 122884
  411.3 12.7 %copy-start.5 = (s32[8]{0:T(128)S(1)}, s32[8]{0:T(128)}, u32[]{:S(2)}) copy-start(s32[8]{0:T(128)} %param.27) | copy-start | bytes 100
  415.8 37.9 %all-to-all-start.3 = ((f32[16,8,4,256]{3,2,1,0:T(4,128)}), f32[16,8,4,256]{3,2,1,0:T(4,128)S(1)}, u32[]{:S(2)}, u32[]{:S(2)}) async-start(f32[16,8,4,256]{3,2,1,0:T(4,128)} %reshape_reshape.3), calls=%async_computation.3 | async-start | bytes 1048576 | tf_op jit(solution)/shard_map/all_to_all | solution.py:51
Sparse Core Ops, SparseCore 0:
  11.6 110.3 all-gather.4
  124.1 63.8 all-gather.2
  207.6 85.7 all-reduce.4
  296.2 93.0 all-reduce.6
where the time goes:
time: 463 us; the launch traced here: 462 us
  waiting for transfers between devices  320 us (69%)
  local copies, waits for them, and re-layouts  53.6 us (12%)
  starting transfers between devices  48.1 us (10%)
  between operations  15.4 us (3%)
  matrix products  15.2 us (3%)
  other arithmetic  10.1 us (2%)
    unnamed x6, waiting for transfers between devices  145 us
    all_gather x1, waiting for transfers between devices, body(): weight_full = lax.all_gather(weight_low, FSDP, axis=0, tiled=True)  68.1 us
    all_gather x1, waiting for transfers between devices, body(): tokens_full = lax.all_gather(hidden, 'tensor', axis=1, tiled=True)  66 us
    unnamed x32, local copies, waits for them, and re-layouts  38.2 us
    all_to_all x2, starting transfers between devices, from_everyone(): lax.all_to_all(jnp.broadcast_to(shard[None], (count, *shard.shape)), axis...  27 us
    all_to_all x1, waiting for transfers between devices, summed_on_arrival(): lax.all_to_all(pieces, axis, split_axis=0, concat_axis=0, tiled=True)  26.3 us
    all_to_all x2, waiting for transfers between devices, from_everyone(): lax.all_to_all(jnp.broadcast_to(shard[None], (count, *shard.shape)), axis...  14.4 us
    all_to_all x1, starting transfers between devices, body(): lax.all_to_all(dec_hidden, FSDP, split_axis=2, concat_axis=0, tiled=True)  14.2 us
  transfers between devices with their start and end apart: 8, of which 7 were waited for; matrix products, arithmetic and copies ran while one was open for 11% of the time, Pallas kernels for 0%

commit v1 on v0

--- a/solution.py
+++ b/solution.py
@@ -143,7 +143,9 @@
     heads_here = kv_width // HD
     head_ratio = QH // KVH
     weight_low = kv_weight.astype(jnp.bfloat16)
-    weight_full = lax.all_gather(weight_low, FSDP, axis=0, tiled=True)
+    weight_full = jnp.concatenate(
+        lax.all_to_all(jnp.stack([weight_low] * lax.axis_size(FSDP)), FSDP, 0, 0), axis=0
+    )
     tokens_full = lax.all_gather(hidden, "tensor", axis=1, tiled=True)
     projected = jnp.dot(
         tokens_full, weight_full.reshape(D, 2 * kv_width), preferred_element_type=jnp.float32

time: 463 us -> 492 us (1.063)
  waiting for transfers between devices: 320 us -> 338 us
  local copies, waits for them, and re-layouts: 53.6 us -> 59.4 us
    all_gather x1, waiting for transfers between devices: 66 us -> 151 us  [body(): tokens_full = lax.all_gather(hidden, 'tensor', axis=1, tiled=True)]
    all_gather x1 -> x0, waiting for transfers between devices: 68.1 us -> none  [body(): weight_full = lax.all_gather(weight_low, FSDP, axis=0, tiled=True)]
    unnamed x32 -> x44, local copies, waits for them, and re-layouts: 38.2 us -> 40.5 us
    unnamed x6 -> x5, waiting for transfers between devices: 145 us -> 143 us
  transfers between devices with their start and end apart: 8 -> 8, of which waited for: 7 -> 6; matrix products, arithmetic and copies ran while one was open for 11% -> 11% of each run, Pallas kernels for 0% -> 0%
where the time goes in v1:
time: 492 us; the launch traced here: 490 us
  waiting for transfers between devices  338 us (69%)
  local copies, waits for them, and re-layouts  59.4 us (12%)
  starting transfers between devices  52.4 us (11%)
  between operations  15.5 us (3%)
  matrix products  14.3 us (3%)
  other arithmetic  10.8 us (2%)
    all_gather x1, waiting for transfers between devices, body(): tokens_full = lax.all_gather(hidden, 'tensor', axis=1, tiled=True)  151 us
    unnamed x5, waiting for transfers between devices  143 us
    unnamed x44, local copies, waits for them, and re-layouts  40.5 us
    all_to_all x2, starting transfers between devices, from_everyone(): lax.all_to_all(jnp.broadcast_to(shard[None], (count, *shard.shape)), axis...  26.7 us
    all_to_all x1, waiting for transfers between devices, summed_on_arrival(): lax.all_to_all(pieces, axis, split_axis=0, concat_axis=0, tiled=True)  26.3 us
    all_to_all x2, waiting for transfers between devices, from_everyone(): lax.all_to_all(jnp.broadcast_to(shard[None], (count, *shard.shape)), axis...  16.7 us
    all_to_all x1, starting transfers between devices, body(): lax.all_to_all(dec_hidden, FSDP, split_axis=2, concat_axis=0, tiled=True)  14.3 us
  transfers between devices with their start and end apart: 8, of which 6 were waited for; matrix products, arithmetic and copies ran while one was open for 11% of the time, Pallas kernels for 0%

profile of v1, /device:TPU:1, one launch (start us, length us, event | category | flops | bytes accessed | tf_op | source)
XLA Modules:
  0.0 490.3 jit_solution(13916811741073370475)
XLA Ops:
  10.1 21.7 %all-to-all-start.1 = ((f32[64,1,128]{2,1,0:T(1,128)}), f32[64,1,128]{2,1,0:T(1,128)S(1)}, u32[]{:S(2)}, u32[]{:S(2)}) async-start(f32[64,1,128]{2,1,0:T(1,128)} %reshape.298), calls=%async_computation.1 | async-start | bytes 65536 | tf_op jit(solution)/shard_map/all_to_all | solution.py:27
  32.9 14.4 %all-to-all-done.1 = f32[64,1,128]{2,1,0:T(1,128)S(1)} async-done(((f32[64,1,128]{2,1,0:T(1,128)}), f32[64,1,128]{2,1,0:T(1,128)S(1)}, u32[]{:S(2)}, u32[]{:S(2)}) %all-to-all-start.1) | async-done | bytes 32800 | tf_op jit(solution)/shard_map/all_to_all | solution.py:27
  47.4 3.5 stack.14
  50.9 3.7 all-to-all-start
  56.8 2.2 copy.157
  59.7 2.1 reduce.7
  64.5 2.1 multiply_convert_fusion.1
  66.6 151.3 %all-gather.2.cloned.1.call-done = bf16[512,5120]{1,0:T(8,128)(2,1)} async-done(((bf16[512,640]{1,0:T(8,128)(2,1)}), bf16[512,5120]{1,0:T(8,128)(2,1)}) %all-gather.2.cloned.1.call-update) | async-done | bytes 5242896 | tf_op jit(solution)/shard_map/all_gather | solution.py:149
  217.9 4.0 fusion.20
  225.9 1.9 fusion
  227.8 2.4 fusion.42
  232.0 4.7 copy.161
  236.7 5.0 %copy.170 = bf16[8,4,5120]{0,1,2:T(4,128)(2,1)} copy(bf16[8,4,5120]{2,1,0:T(4,128)(2,1)S(1)} %copy-done.5) | data formatting | bytes 655360 | tf_op args[10]
  241.7 12.3 %reshape.300 = bf16[16,2,5120]{2,1,0:T(2,128)(2,1)} reshape(bf16[5120,4,8]{2,1,0:T(4,128)(2,1)} %bitcast.238) | data formatting | bytes 655360
  254.0 14.3 %all-to-all-start.3 = ((bf16[16,2,5120]{2,1,0:T(2,128)(2,1)}), bf16[16,2,5120]{2,1,0:T(2,128)(2,1)S(1)}, u32[]{:S(2)}, u32[]{:S(2)}) async-start(bf16[16,2,5120]{2,1,0:T(2,128)(2,1)} %reshape.300), calls=%async_computation.3 | async-start | bytes 655360 | tf_op jit(solution)/shard_map/all_to_all | solution.py:197
  270.2 50.7 %all-reduce.5.cloned.1.call-done = bf16[5120,2,128]{2,1,0:T(2,128)(2,1)} async-done(((bf16[5120,2,128]{2,1,0:T(2,128)(2,1)}), bf16[5120,2,128]{2,1,0:T(2,128)(2,1)}) %all-reduce.5.cloned.1.call-update) | async-done | bytes 2621456
  321.0 2.2 constant_dynamic-slice_fusion.1
  325.1 92.0 %all-reduce.7.cloned.1.call-done = bf16[1280,2,128]{2,1,0:T(2,128)(2,1)} async-done(((bf16[1280,2,128]{2,1,0:T(2,128)(2,1)}), bf16[1280,2,128]{2,1,0:T(2,128)(2,1)}) %all-reduce.7.cloned.1.call-update) | async-done | bytes 655376
  419.4 4.9 %all-to-all-start.2 = ((f32[4,320,2,128]{3,1,2,0:T(8,128)}), f32[4,320,2,128]{3,1,2,0:T(8,128)S(1)}, u32[]{:S(2)}, u32[]{:S(2)}) async-start(f32[4,320,2,128]{3,1,2,0:T(8,128)} %broadcast_in_dim.31), calls=%async_computation.2 | async-start | bytes 2621440 | tf_op jit(solution)/shard_map/all_to_all | solution.py:27
  424.3 7.2 %reshape.301 = bf16[5120,4,8]{2,1,0:T(4,128)(2,1)} reshape(bf16[16,2,5120]{2,1,0:T(2,128)(2,1)S(1)} %all-to-all-done.3) | data formatting | bytes 655360
  431.5 7.0 %copy.171 = bf16[8,4,16,320]{3,1,0,2:T(4,128)(2,1)S(1)} copy(bf16[8,4,16,320]{0,1,3,2:T(4,128)(2,1)} %bitcast.237) | data formatting | bytes 655360 | tf_op jit(solution)/shard_map/all_to_all | solution.py:197
  438.7 2.3 all-to-all-done.2
  442.9 7.6 %all-to-all-start.4 = ((f32[16,8,4,256]{3,2,1,0:T(4,128)}), f32[16,8,4,256]{3,2,1,0:T(4,128)S(1)}, u32[]{:S(2)}, u32[]{:S(2)}) async-start(f32[16,8,4,256]{3,2,1,0:T(4,128)} %reshape_reshape.7), calls=%async_computation.4 | async-start | bytes 1048576 | tf_op jit(solution)/shard_map/all_to_all | solution.py:51
  455.4 26.3 %all-to-all-done.4 = f32[16,8,4,256]{3,2,1,0:T(4,128)S(1)} async-done(((f32[16,8,4,256]{3,2,1,0:T(4,128)}), f32[16,8,4,256]{3,2,1,0:T(4,128)S(1)}, u32[]{:S(2)}, u32[]{:S(2)}) %all-to-all-start.4) | async-done | bytes 524320 | tf_op jit(solution)/shard_map/all_to_all | solution.py:51
  (91 shorter events, 28.8 us)
Async XLA Ops:
  10.1 37.3 %all-to-all-start.1 = ((f32[64,1,128]{2,1,0:T(1,128)}), f32[64,1,128]{2,1,0:T(1,128)S(1)}, u32[]{:S(2)}, u32[]{:S(2)}) async-start(f32[64,1,128]{2,1,0:T(1,128)} %reshape.298), calls=%async_computation.1 | async-start | bytes 65536 | tf_op jit(solution)/shard_map/all_to_all | solution.py:27
  32.9 26.1 %copy-start.8 = (s32[1,512]{1,0:T(1,128)S(1)}, s32[1,512]{1,0:T(1,128)}, u32[]{:S(2)}) copy-start(s32[1,512]{1,0:T(1,128)} %param.17) | copy-start | bytes 6148
  32.9 31.5 %copy-start.10 = (f32[16]{0:T(128)S(1)}, f32[16]{0:T(128)}, u32[]{:S(2)}) copy-start(f32[16]{0:T(128)} %param.19) | copy-start | bytes 196
  32.9 31.6 %copy-start.9 = (s32[512]{0:T(512)S(1)}, s32[512]{0:T(512)}, u32[]{:S(2)}) copy-start(s32[512]{0:T(512)} %param.18) | copy-start | bytes 6148
  47.4 8.0 %copy-start.6 = (f32[64,1,128]{2,1,0:T(1,128)}, f32[64,1,128]{2,1,0:T(1,128)S(1)}, u32[]{:S(2)}) copy-start(f32[64,1,128]{2,1,0:T(1,128)S(1)} %all-to-all-done.1) | copy-start | bytes 98308
  50.9 167.0 %all-to-all-start = ((bf16[16,320,2,128]{3,2,1,0:T(2,128)(2,1)}), bf16[16,320,2,128]{3,2,1,0:T(2,128)(2,1)S(1)}, u32[]{:S(2)}, u32[]{:S(2)}) async-start(bf16[16,320,2,128]{3,2,1,0:T(2,128)(2,1)} %stack.14), calls=%async_computation | async-start | bytes 5242880 | tf_op jit(solution)/shard_map/all_to_all | solution.py:147
  54.6 163.3 %all-gather.2.cloned.1.call-start = ((), (), s32[]{:S(2)}) async-start(), calls=%async_computation.5 | async-start | bytes 5898240 | tf_op jit(solution)/shard_map/all_gather | solution.py:149
  55.4 265.6 %all-reduce.5.cloned.1.call-start = ((), (), s32[]{:S(2)}) async-start(), calls=%async_computation.6 | async-start | bytes 5242880
  222.0 2.2 copy-start
  224.2 1.7 copy-start.2
  225.9 4.4 slice-start
  227.8 2.5 slice-start.1
  231.9 4.8 copy-start.5
  254.0 164.2 %all-to-all-start.3 = ((bf16[16,2,5120]{2,1,0:T(2,128)(2,1)}), bf16[16,2,5120]{2,1,0:T(2,128)(2,1)S(1)}, u32[]{:S(2)}, u32[]{:S(2)}) async-start(bf16[16,2,5120]{2,1,0:T(2,128)(2,1)} %reshape.300), calls=%async_computation.3 | async-start | bytes 655360 | tf_op jit(solution)/shard_map/all_to_all | solution.py:197
  268.3 148.8 %all-reduce.7.cloned.1.call-start = ((), (), s32[]{:S(2)}) async-start(), calls=%async_computation.7 | async-start | bytes 1310720
  419.4 21.7 %all-to-all-start.2 = ((f32[4,320,2,128]{3,1,2,0:T(8,128)}), f32[4,320,2,128]{3,1,2,0:T(8,128)S(1)}, u32[]{:S(2)}, u32[]{:S(2)}) async-start(f32[4,320,2,128]{3,1,2,0:T(8,128)} %broadcast_in_dim.31), calls=%async_computation.2 | async-start | bytes 2621440 | tf_op jit(solution)/shard_map/all_to_all | solution.py:27
  431.5 9.6 %copy-start.1 = (f32[320,2,128]{2,1,0:T(2,128)S(1)}, f32[320,2,128]{2,1,0:T(2,128)}, u32[]{:S(2)}) copy-start(f32[320,2,128]{2,1,0:T(2,128)} %param.21) | copy-start | bytes 983044
  431.5 9.6 %copy-start.3 = (f32[320,2,128]{2,1,0:T(2,128)S(1)}, f32[320,2,128]{2,1,0:T(2,128)}, u32[]{:S(2)}) copy-start(f32[320,2,128]{2,1,0:T(2,128)} %param.22) | copy-start | bytes 983044
  431.5 9.6 %copy-start.4 = (f32[320,2,128]{2,1,0:T(2,128)S(1)}, f32[320,2,128]{2,1,0:T(2,128)}, u32[]{:S(2)}) copy-start(f32[320,2,128]{2,1,0:T(2,128)} %param.23) | copy-start | bytes 983044
  438.5 12.0 %copy-start.7 = (bf16[8,4,640]{2,1,0:T(4,128)(2,1)S(1)}, bf16[8,4,640]{2,1,0:T(4,128)(2,1)}, u32[]{:S(2)}) copy-start(bf16[8,4,640]{2,1,0:T(4,128)(2,1)} %param.25) | copy-start | bytes 122884
  438.7 13.3 %copy-start.11 = (s32[8]{0:T(128)S(1)}, s32[8]{0:T(128)}, u32[]{:S(2)}) copy-start(s32[8]{0:T(128)} %param.27) | copy-start | bytes 100
  442.9 38.8 %all-to-all-start.4 = ((f32[16,8,4,256]{3,2,1,0:T(4,128)}), f32[16,8,4,256]{3,2,1,0:T(4,128)S(1)}, u32[]{:S(2)}, u32[]{:S(2)}) async-start(f32[16,8,4,256]{3,2,1,0:T(4,128)} %reshape_reshape.7), calls=%async_computation.4 | async-start | bytes 1048576 | tf_op jit(solution)/shard_map/all_to_all | solution.py:51
Sparse Core Ops, SparseCore 0:
  57.5 160.3 all-gather.1
  236.8 84.1 all-reduce.4
  323.9 93.1 all-reduce.6
